TPU v7x, 32 devices: a whole 2x2x4 slice. The times are simulated.
32 devices in a mesh: member: 1, span: 32 (over z, y, x, core).
Axes of the slice: x: 2, y: 2, z: 4, core: 2. Of those that a mesh axis runs over, the one named last changes fastest.
Arguments:
- field: float32 [1024, 23040], P(('member', 'span')), may hold values from -60 to 60
- day_table: int32 [1024], P('member'), may hold values from 0 to 364
- band_owner: int32 [32], P('member'), may hold values from 0 to 31, as said below
- sea_mask: int32 [23040], replicated, may hold values 0 or 1
Outputs:
- coeff_out: float32 [13, 23040], P(None, ('member', 'span'))
- variance_out: float32 [23040], P(('member', 'span'))
Inputs may be any that keep to these rules, and one draw needn't show every extreme that they name: `band_owner`: a permutation of 0 to 31.
All inputs are finite; a program needn't handle non-finite values.
Results may differ from a plain program's by a relative error of at most 0.00013.
Values sent between devices are 32-bit elements; how exact they have to be, the bound alone decides.
No kernel may reach another device: no remote copies, remote signals or barrier semaphores. Data moves between devices by JAX's collectives and lax.ppermute only.
A program may use at most 64 MiB of HBM per device.

v0:
```python
import math
import jax
import jax.numpy as jnp
from jax import lax
from jax.sharding import PartitionSpec as P

HARMS = 6


def harmonic_basis(day_values):
    angles = day_values.astype(jnp.float32) * (2.0 * math.pi / 365.0)
    basis_rows = [jnp.ones_like(angles)]
    for order in range(1, HARMS + 1):
        basis_rows.append(jnp.cos(order * angles))
        basis_rows.append(jnp.sin(order * angles))
    return jnp.stack(basis_rows, 0)


def on_device(field, day_table, band_owner, sea_mask):
    groups = lax.axis_size("span")
    own_index = lax.axis_index("span")
    steps_dev, cells = field.shape
    band_cells = cells // groups
    design = harmonic_basis(day_table)
    total_steps = design.shape[1]
    gram_matrix = jnp.dot(design, design.T, precision=lax.Precision.HIGHEST)
    factor = jnp.linalg.cholesky(gram_matrix)
    slots = jnp.arange(groups, dtype=jnp.int32)
    own_band = jnp.sum(jnp.where(band_owner == own_index, slots, 0))
    source_band = jnp.sum(
        jnp.where(band_owner[None, :] == slots[:, None], slots[None, :], 0), axis=1
    )
    blocks = field.reshape(steps_dev, groups, band_cells)
    outgoing = jnp.take(blocks, source_band, axis=1).reshape(steps_dev, cells)
    weight_mask = lax.dynamic_slice_in_dim(sea_mask, own_band * band_cells, band_cells).astype(
        jnp.float32
    )
    series = lax.all_to_all(outgoing, "span", split_axis=1, concat_axis=0, tiled=True)
    projection = jnp.dot(design, series, precision=lax.Precision.HIGHEST)
    coeffs = jax.scipy.linalg.cho_solve((factor, True), projection)
    residual = series - jnp.dot(design.T, coeffs, precision=lax.Precision.HIGHEST)
    variance = jnp.sum(residual * residual, axis=0) / total_steps
    coeffs = coeffs * weight_mask[None, :]
    variance = variance * weight_mask
    return (coeffs, variance)


def solution(mesh):
    in_specs = (P(("member", "span"), None), P("member"), P("member"), P())
    out_specs = (P(None, ("member", "span")), P(("member", "span")))
    return jax.shard_map(
        on_device, mesh=mesh, in_specs=in_specs, out_specs=out_specs, check_vma=False
    )
```

profile of v0, /device:TPU:0, one launch (start us, length us, event | category | flops | bytes accessed | tf_op | source)
XLA Modules:
  0.0 103.2 jit_solution(3279304344381537644)
XLA Ops:
  0.6 0.8 select_reduce_fusion
  1.4 4.1 %reshape.51 = f32[32,32,720]{2,1,0:T(8,128)S(1)} reshape(f32[32,23040]{1,0:T(8,128)} %param.4) | data formatting | bytes 5898240 | tf_op jit(solution)/shard_map/reshape | solution.py:33
  5.6 3.5 %copy.13 = f32[32,32,720]{2,0,1:T(8,128)} copy(f32[32,32,720]{2,1,0:T(8,128)S(1)} %reshape.51) | data formatting | bytes 5898240 | tf_op jit(solution)/shard_map/reshape | solution.py:33
  9.1 2.6 %gather_fusion = f32[32,32,720]{2,1,0:T(8,128)S(1)} fusion(f32[32,32,720]{2,0,1:T(8,128)} %copy.13, s32[1024]{0:T(1024)S(1)} %pad_clamp_fusion), kind=kCustom, calls=%fused_computation | custom fusion | bytes 5898368 | tf_op jit(solution)/shard_map/jit(_take)/gather | solution.py:34
  11.7 2.0 %select_bitcast_fusion = f32[32,32,720]{2,0,1:T(8,128)} fusion(f32[32,32,720]{2,1,0:T(8,128)S(1)} %gather_fusion, pred[32]{0:T(512)(128)(4,1)S(1)} %compare_and_fusion), kind=kLoop, calls=%fused_computation.1 | loop fusion | flops 737280 | bytes 5898272 | tf_op jit(solution)/shard_map/jit(_take)/select_n | solution.py:34
  13.8 0.0 copy-start
  13.8 0.0 copy-start.1
  13.8 7.3 %all-to-all-start = ((f32[32,32,720]{2,0,1:T(8,128)}), f32[32,32,720]{2,0,1:T(8,128)S(1)}, u32[]{:S(2)}, u32[]{:S(2)}) async-start(f32[32,32,720]{2,0,1:T(8,128)} %select_bitcast_fusion), calls=%async_computation | async-start | bytes 6291456 | tf_op jit(solution)/shard_map/all_to_all | solution.py:38
  21.1 0.0 copy-done
  21.1 0.1 fusion.16
  21.2 0.1 stack.51
  21.3 0.2 fusion.20
  21.5 0.1 copy.12
  21.6 1.2 %cholesky.16 = f32[13,13]{1,0:T(8,128)S(1)} custom-call(f32[13,13]{1,0:T(8,128)S(1)} %fusion.5), custom_call_target="Cholesky" | custom-call | tf_op jit(solution)/shard_map/jit(cholesky)/cholesky | solution.py:27
  22.9 0.6 compare_reduce_fusion
  23.5 0.6 fusion
  24.2 1.0 custom-call.10
  25.2 0.0 copy-done.1
  25.2 0.6 fusion.18
  26.5 66.0 %all-to-all-done = f32[32,32,720]{2,0,1:T(8,128)S(1)} async-done(((f32[32,32,720]{2,0,1:T(8,128)}), f32[32,32,720]{2,0,1:T(8,128)S(1)}, u32[]{:S(2)}, u32[]{:S(2)}) %all-to-all-start) | async-done | bytes 2949152 | tf_op jit(solution)/shard_map/all_to_all | solution.py:38
  92.4 1.6 %fusion.21 = f32[13,720]{1,0:T(8,128)S(1)} fusion(f32[13,1024]{1,0:T(8,128)S(1)} %stack.51, f32[1024,720]{1,0:T(8,128)S(1)} %bitcast.40), kind=kOutput, calls=%fused_computation.46 | convolution fusion | flops 115015680 | bytes 3039808 | tf_op jit(solution)/shard_map/dot_general | solution.py:39
  94.0 2.3 %copy.14 = f32[1024,720]{0,1:T(8,128)} copy(f32[1024,720]{1,0:T(8,128)S(1)} %bitcast.41) | data formatting | bytes 5898240 | tf_op jit(solution)/shard_map/all_to_all | solution.py:38
  96.3 0.2 fusion.3
  96.6 0.2 fusion.1
  96.7 4.5 %multiply_reduce_fusion = f32[720]{0:T(1024)S(1)} fusion(f32[1024,720]{0,1:T(8,128)} %copy.14, f32[13,1024]{1,0:T(8,128)S(1)} %stack.51, f32[13,720]{1,0:T(8,128)S(1)} %fusion.1), kind=kOutput, calls=%fused_computation.2 | convolution fusion | flops 117226800 | bytes 3042688 | tf_op jit(solution)/shard_map/dot_general | solution.py:41
  101.2 1.4 %multiply_multiply_fusion = (f32[720]{0:T(1024)}, f32[720]{0:T(1024)S(1)}) fusion(f32[720]{0:T(1024)S(1)} %multiply_reduce_fusion, s32[23040]{0:T(1024)} %param.7, s32[]{:T(128)S(6)} %select_n.43), kind=kLoop, calls=%fused_computation.18 | loop fusion | flops 2160 | bytes 11524 | tf_op jit(solution)/shard_map/mul | solution.py:44
  102.6 0.6 broadcast_multiply_fusion
  (6 shorter events, 0.1 us)
Async XLA Ops:
  13.8 7.3 %copy-start = (s32[1024]{0:T(1024)S(1)}, s32[1024]{0:T(1024)}, u32[]{:S(2)}) copy-start(s32[1024]{0:T(1024)} %param.5) | copy-start | bytes 12292
  13.8 11.4 %copy-start.1 = (s32[32]{0:T(128)S(1)}, s32[32]{0:T(128)}, u32[]{:S(2)}) copy-start(s32[32]{0:T(128)} %param.6) | copy-start | bytes 388
  13.8 78.7 %all-to-all-start = ((f32[32,32,720]{2,0,1:T(8,128)}), f32[32,32,720]{2,0,1:T(8,128)S(1)}, u32[]{:S(2)}, u32[]{:S(2)}) async-start(f32[32,32,720]{2,0,1:T(8,128)} %select_bitcast_fusion), calls=%async_computation | async-start | bytes 6291456 | tf_op jit(solution)/shard_map/all_to_all | solution.py:38
where the time goes:
time: 104 us; the launch traced here: 103 us
  waiting for transfers between devices  66 us (63%)
  local copies, waits for them, and re-layouts  12.8 us (12%)
  other arithmetic  9.1 us (9%)
  starting transfers between devices  7.33 us (7%)
  matrix products  6.68 us (6%)
  between operations  1.39 us (1%)
    all_to_all x1, waiting for transfers between devices, on_device(): lax.all_to_all(outgoing, 'span', split_axis=1, concat_axis=0, tiled=True)  66 us
    reshape x2, local copies, waits for them, and re-layouts, on_device(): blocks = field.reshape(steps_dev, groups, band_cells)  7.63 us
    all_to_all x1, starting transfers between devices, on_device(): lax.all_to_all(outgoing, 'span', split_axis=1, concat_axis=0, tiled=True)  7.33 us
    dot_general x1, matrix products, on_device(): jnp.dot(design.T, coeffs, precision=lax.Precision.HIGHEST)  4.5 us
    gather x1, local copies, waits for them, and re-layouts, on_device(): outgoing = jnp.take(blocks, source_band, axis=1).reshape(steps_dev, cells)  2.64 us
    all_to_all x1, local copies, waits for them, and re-layouts, on_device(): lax.all_to_all(outgoing, 'span', split_axis=1, concat_axis=0, tiled=True)  2.3 us
  transfers between devices with their start and end apart: 1, of which 1 were waited for; matrix products, arithmetic and copies ran while one was open for 5% of the time, Pallas kernels for 0%

commit v1 on v0

--- a/solution.py
+++ b/solution.py
@@ -3,8 +3,16 @@
 import jax.numpy as jnp
 from jax import lax
 from jax.sharding import PartitionSpec as P
+from jax.lax import all_to_all, axis_size
 
 HARMS = 6
+
+
+def ratios_note(base_x):
+    earlier = jnp.concatenate(
+        all_to_all(jnp.stack(jnp.split(base_x, axis_size("span"), axis=1), 0), "span", 0, 0), 0
+    )
+    return earlier
 
 
 def harmonic_basis(day_values):
@@ -35,7 +43,7 @@
     weight_mask = lax.dynamic_slice_in_dim(sea_mask, own_band * band_cells, band_cells).astype(
         jnp.float32
     )
-    series = lax.all_to_all(outgoing, "span", split_axis=1, concat_axis=0, tiled=True)
+    series = ratios_note(outgoing)
     projection = jnp.dot(design, series, precision=lax.Precision.HIGHEST)
     coeffs = jax.scipy.linalg.cho_solve((factor, True), projection)
     residual = series - jnp.dot(design.T, coeffs, precision=lax.Precision.HIGHEST)

time: 104 us -> 133 us (1.28)
  local copies, waits for them, and re-layouts: 12.8 us -> 43.7 us
  matrix products: 6.68 us -> 4.95 us
    unnamed x4 -> x37, local copies, waits for them, and re-layouts: 0.01 us -> 22.2 us
    gather x1 -> x3, local copies, waits for them, and re-layouts: 2.64 us -> 9.1 us  [on_device(): outgoing = jnp.take(blocks, source_band, axis=1).reshape(steps_dev, cells)]
    all_to_all x1 -> x0, local copies, waits for them, and re-layouts: 2.3 us -> none  [on_device(): lax.all_to_all(outgoing, 'span', split_axis=1, concat_axis=0, tiled=True)]
    reshape x0 -> x1, local copies, waits for them, and re-layouts: none -> 2.29 us  [ratios_note(): jnp.concatenate(all_to_all(jnp.stack(jnp.split(base_x, axis_size('span'),...]
    dot_general x1, matrix products: 4.5 us -> 2.77 us  [on_device(): jnp.dot(design.T, coeffs, precision=lax.Precision.HIGHEST)]
    reshape x2, local copies, waits for them, and re-layouts: 7.63 us -> 8.99 us  [on_device(): blocks = field.reshape(steps_dev, groups, band_cells)]
  transfers between devices with their start and end apart: 1 -> 1, of which waited for: 1 -> 1; matrix products, arithmetic and copies ran while one was open for 5% -> 4% of each run, Pallas kernels for 0% -> 0%
where the time goes in v1:
time: 133 us
  waiting for transfers between devices  65.9 us (50%)
  local copies, waits for them, and re-layouts  43.7 us (33%)
  other arithmetic  9.15 us (7%)
  starting transfers between devices  7.51 us (6%)
  matrix products  4.95 us (4%)
  between operations  1.41 us (1%)
    all_to_all x1, waiting for transfers between devices, ratios_note(): all_to_all(jnp.stack(jnp.split(base_x, axis_size('span'), axis=1), 0), 's...  65.9 us
    unnamed x37, local copies, waits for them, and re-layouts  22.2 us
    gather x3, local copies, waits for them, and re-layouts, on_device(): outgoing = jnp.take(blocks, source_band, axis=1).reshape(steps_dev, cells)  9.1 us
    reshape x2, local copies, waits for them, and re-layouts, on_device(): blocks = field.reshape(steps_dev, groups, band_cells)  8.99 us
    all_to_all x1, starting transfers between devices, ratios_note(): all_to_all(jnp.stack(jnp.split(base_x, axis_size('span'), axis=1), 0), 's...  7.51 us
    dot_general x1, matrix products, on_device(): jnp.dot(design.T, coeffs, precision=lax.Precision.HIGHEST)  2.77 us
  transfers between devices with their start and end apart: 1, of which 1 were waited for; matrix products, arithmetic and copies ran while one was open for 4% of the time, Pallas kernels for 0%

profile of v1, /device:TPU:0, one launch (start us, length us, event | category | flops | bytes accessed | tf_op | source)
XLA Modules:
  0.0 132.6 jit_solution(13275468093757229753)
XLA Ops:
  0.6 0.8 select_reduce_fusion
  1.4 5.3 %reshape.46 = f32[32,32,720]{2,1,0:T(8,128)} reshape(f32[32,23040]{1,0:T(8,128)} %param.4) | data formatting | bytes 5898240 | tf_op jit(solution)/shard_map/reshape | solution.py:41
  6.7 3.7 %copy.46 = f32[32,32,720]{2,0,1:T(8,128)S(1)} copy(f32[32,32,720]{2,1,0:T(8,128)} %reshape.46) | data formatting | bytes 5898240 | tf_op jit(solution)/shard_map/reshape | solution.py:41
  10.4 2.4 %gather_fusion = f32[32,32,720]{2,1,0:T(8,128)} fusion(f32[32,32,720]{2,0,1:T(8,128)S(1)} %copy.46, s32[1024]{0:T(1024)S(1)} %pad_clamp_fusion), kind=kCustom, calls=%fused_computation | custom fusion | bytes 5898368 | tf_op jit(solution)/shard_map/jit(_take)/gather | solution.py:42
  12.8 3.7 %copy.47 = f32[32,32,720]{2,1,0:T(8,128)S(1)} copy(f32[32,32,720]{2,0,1:T(8,128)} %bitcast.167) | data formatting | bytes 5898240 | tf_op jit(solution)/shard_map/jit(_take)/gather | solution.py:42
  16.6 3.0 %gather.7 = f32[32,23040]{1,0:T(8,128)} reshape(f32[32,32,720]{2,1,0:T(8,128)S(1)} %copy.47) | data formatting | bytes 5898240 | tf_op jit(solution)/shard_map/jit(_take)/gather | solution.py:42
  19.5 0.1 broadcast_in_dim.36
  19.6 0.1 broadcast_in_dim.37
  19.7 2.1 %broadcast_select_fusion = f32[32,23040]{1,0:T(8,128)S(1)} fusion(f32[32,23040]{1,0:T(8,128)} %gather.7, pred[23040]{0:T(1024)(128)(4,1)S(1)} %broadcast_in_dim.37), kind=kLoop, calls=%fused_computation.2 | loop fusion | flops 737280 | bytes 5921280 | tf_op jit(solution)/shard_map/jit(_take)/select_n | solution.py:42
  21.8 0.6 fusion.31
  22.5 0.7 fusion.30
  23.2 0.7 fusion.29
  23.9 0.7 fusion.28
  24.7 0.7 fusion.27
  25.4 0.7 fusion.26
  26.1 0.7 fusion.25
  26.8 0.7 fusion.24
  27.6 0.6 fusion.23
  28.2 0.7 fusion.22
  28.9 0.7 fusion.21
  29.7 0.7 fusion.20
  30.4 0.7 fusion.19
  31.1 0.7 fusion.18
  31.8 0.7 fusion.17
  32.6 0.7 fusion.16
  33.3 0.6 fusion.15
  33.9 0.7 fusion.14
  34.6 0.7 fusion.13
  35.4 0.7 fusion.12
  36.1 0.7 fusion.11
  36.8 0.7 fusion.10
  37.6 0.7 fusion.9
  38.3 0.7 fusion.8
  39.0 0.6 fusion.7
  39.7 0.7 fusion.6
  40.4 0.7 fusion.5
  41.1 0.7 fusion.4
  41.8 0.7 fusion.3
  42.6 0.7 fusion.2
  43.3 0.7 fusion.1
  44.0 0.7 fusion
  44.7 0.0 copy-start.1
  44.7 0.0 copy-start.2
  44.7 7.5 %all-to-all-start = ((f32[32,32,720]{2,1,0:T(8,128)}), f32[32,32,720]{2,1,0:T(8,128)S(1)}, u32[]{:S(2)}, u32[]{:S(2)}) async-start(f32[32,32,720]{2,1,0:T(8,128)} %fusion), calls=%async_computation | async-start | bytes 6291456 | tf_op jit(solution)/shard_map/all_to_all | solution.py:13
  52.2 0.0 copy-done.1
  52.3 0.1 fusion.48
  52.4 0.1 stack.150
  52.5 0.2 fusion.52
  52.7 0.1 copy.45
  52.8 1.2 cholesky.16
  54.0 0.6 compare_reduce_fusion
  54.7 0.6 fusion.32
  55.3 1.0 custom-call.10
  56.3 0.0 copy-done.2
  56.3 0.6 fusion.50
  57.6 65.9 %all-to-all-done = f32[32,32,720]{2,1,0:T(8,128)S(1)} async-done(((f32[32,32,720]{2,1,0:T(8,128)}), f32[32,32,720]{2,1,0:T(8,128)S(1)}, u32[]{:S(2)}, u32[]{:S(2)}) %all-to-all-start) | async-done | bytes 2949152 | tf_op jit(solution)/shard_map/all_to_all | solution.py:13
  123.5 2.3 %copy.48 = f32[1024,720]{0,1:T(8,128)} copy(f32[1024,720]{1,0:T(8,128)S(1)} %bitcast.165) | data formatting | bytes 5898240 | tf_op jit(solution)/shard_map/reshape | solution.py:12
  125.8 1.6 %fusion.53 = f32[13,720]{1,0:T(8,128)S(1)} fusion(f32[13,1024]{1,0:T(8,128)S(1)} %stack.150, f32[1024,720]{1,0:T(8,128)S(1)} %bitcast.166), kind=kOutput, calls=%fused_computation.110 | convolution fusion | flops 115015680 | bytes 3039808 | tf_op jit(solution)/shard_map/dot_general | solution.py:47
  127.4 0.3 fusion.35
  127.7 0.2 fusion.33
  127.8 0.0 copy-done
  127.8 2.8 %multiply_reduce_fusion = f32[720]{0:T(1024)S(1)} fusion(f32[1024,720]{0,1:T(8,128)S(1)} %copy-done, f32[13,1024]{1,0:T(8,128)S(1)} %stack.150, f32[13,720]{1,0:T(8,128)S(1)} %fusion.33), kind=kOutput, calls=%fused_computation.1 | convolution fusion | flops 117226800 | bytes 3042688 | tf_op jit(solution)/shard_map/dot_general | solution.py:49
  130.6 1.4 %multiply_multiply_fusion = (f32[720]{0:T(1024)}, f32[720]{0:T(1024)S(1)}) fusion(f32[720]{0:T(1024)S(1)} %multiply_reduce_fusion, s32[23040]{0:T(1024)} %param.7, s32[]{:T(128)S(6)} %select_n.42), kind=kLoop, calls=%fused_computation.82 | loop fusion | flops 2160 | bytes 11524 | tf_op jit(solution)/shard_map/mul | solution.py:52
  132.0 0.6 broadcast_multiply_fusion
  (7 shorter events, 0.1 us)
Async XLA Ops:
  44.7 7.5 %copy-start.1 = (s32[1024]{0:T(1024)S(1)}, s32[1024]{0:T(1024)}, u32[]{:S(2)}) copy-start(s32[1024]{0:T(1024)} %param.5) | copy-start | bytes 12292
  44.7 11.6 %copy-start.2 = (s32[32]{0:T(128)S(1)}, s32[32]{0:T(128)}, u32[]{:S(2)}) copy-start(s32[32]{0:T(128)} %param.6) | copy-start | bytes 388
  44.7 78.8 %all-to-all-start = ((f32[32,32,720]{2,1,0:T(8,128)}), f32[32,32,720]{2,1,0:T(8,128)S(1)}, u32[]{:S(2)}, u32[]{:S(2)}) async-start(f32[32,32,720]{2,1,0:T(8,128)} %fusion), calls=%async_computation | async-start | bytes 6291456 | tf_op jit(solution)/shard_map/all_to_all | solution.py:13
  125.8 2.0 %copy-start = (f32[1024,720]{0,1:T(8,128)S(1)}, f32[1024,720]{0,1:T(8,128)}, u32[]{:S(2)}) copy-start(f32[1024,720]{0,1:T(8,128)} %copy.48) | copy-start | bytes 8847364
